TPU v7x, 32 devices: a whole 2x2x4 slice. The times are simulated.
32 devices in a mesh: branch: 2 (over x), batch: 4 (over y, core), rows: 4 (over z).
Axes of the slice: x: 2, y: 2, z: 4, core: 2. Of those that a mesh axis runs over, the one named last changes fastest.
Arguments:
- timestep: int32 [4], P('batch'), parts along dimension 0, may hold values from 0 to 999
- features: bfloat16 [4, 2, 32, 64, 640], P('batch', 'branch', 'rows'), parts along dimension 0, may hold values from -6 to 6
- conv1_weight: bfloat16 [2, 3, 3, 640, 640], P('branch', None, None, None, 'rows'), may hold values from -0.078125 to 0.078125
- conv1_bias: float32 [2, 640], P('branch'), may hold values from -3 to 3
- conv2_weight: bfloat16 [2, 3, 3, 640, 640], P('branch', None, None, None, 'rows'), may hold values from -0.078125 to 0.078125
- conv2_bias: float32 [2, 640], P('branch'), may hold values from -3 to 3
- norm1_gain: float32 [2, 640], P('branch'), may hold values from 0.25 to 1.75
- norm1_shift: float32 [2, 640], P('branch'), may hold values from -3 to 3
- norm2_gain: float32 [2, 640], P('branch'), may hold values from 0.25 to 1.75
- norm2_shift: float32 [2, 640], P('branch'), may hold values from -3 to 3
- time_weight: bfloat16 [2, 320, 1280], P('branch'), may hold values from -0.3125 to 0.3125
- emb_weight: bfloat16 [2, 1280, 640], P('branch'), may hold values from -0.15625 to 0.15625
- zero_weight: bfloat16 [640, 640], replicated, may hold values from -0.25 to 0.25
- zero_bias: float32 [640], replicated, may hold values from -3 to 3
Outputs:
- block_out: bfloat16 [4, 2, 32, 64, 640], P('batch', 'branch', 'rows'), parts along dimension 0
There are 4 independent parts, one for each index of `batch`. A program takes and returns all parts, laid end to end along the dimension named above; an argument that names none is the same for every part. Nothing has to cross between parts.
All inputs are finite; a program needn't handle non-finite values.
Results may differ from a plain program's by a relative error of at most 0.01.
Values may be sent and summed in bfloat16 or wider, within the bound.
A program may use at most 128 MiB of HBM per device.

v0:
```python
import math

import jax
import jax.numpy as jnp
from jax import lax
from jax.sharding import PartitionSpec as P

GROUPS = 32


def as_sent(x):

    def short(part):
        return part.astype(jnp.bfloat16) if part.dtype == jnp.float32 else part

    return jax.tree.map(short, x)


def from_behind(x, axis, by):
    length = lax.axis_size(axis)
    pairs = [(i, i + by) for i in range(length) if 0 <= i + by < length]
    return lax.ppermute(x, axis, pairs)


def sinusoid(timestep, count):
    half = count // 2
    freqs = jnp.exp(-math.log(10000.0) * jnp.arange(half, dtype=jnp.float32) / half)
    angles = timestep.astype(jnp.float32)[0] * freqs
    return jnp.concatenate([jnp.cos(angles), jnp.sin(angles)])


def time_shift(timestep, time_weight, emb_weight):
    waves = sinusoid(timestep, time_weight.shape[0])
    inner = jax.nn.silu(
        jnp.dot(waves, time_weight.astype(jnp.float32), precision=lax.Precision.HIGHEST)
    )
    return jnp.dot(inner, emb_weight.astype(jnp.float32), precision=lax.Precision.HIGHEST)


def group_sums(values, groups):
    rows, cols, chans = values.shape
    grouped = values.reshape(rows, cols, groups, chans // groups)
    return (jnp.sum(grouped, axis=(0, 1, 3)), jnp.sum(grouped * grouped, axis=(0, 1, 3)))


def apply_norm(values, total, square, count, gain, shift):
    rows, cols, chans = values.shape
    groups = total.shape[0]
    mean = total / count
    var = square / count - mean * mean
    grouped = values.reshape(rows, cols, groups, chans // groups)
    normed = (grouped - mean[:, None]) * lax.rsqrt(var + 1e-05)[:, None]
    return jax.nn.silu(normed.reshape(values.shape) * gain + shift).astype(jnp.bfloat16)


def convolve(inputs, kernel, padding):
    return lax.conv_general_dilated(
        inputs[None],
        kernel,
        (1, 1),
        padding,
        dimension_numbers=("NHWC", "HWIO", "NHWC"),
        preferred_element_type=jnp.float32,
    )[0]


def body(
    timestep,
    features,
    conv1_weight,
    conv1_bias,
    conv2_weight,
    conv2_bias,
    norm1_gain,
    norm1_shift,
    norm2_gain,
    norm2_shift,
    time_weight,
    emb_weight,
    zero_weight,
    zero_bias,
):
    inputs = features[0, 0]
    rows_here, width, chans = inputs.shape
    parts = lax.axis_size("rows")
    full = rows_here * parts
    per_group = chans // GROUPS
    count = full * width * per_group
    extra = time_shift(timestep, time_weight[0], emb_weight[0])
    quarter = conv1_weight.shape[4]
    first = lax.axis_index("rows") * quarter

    def mine(vector):
        return lax.dynamic_slice_in_dim(vector, first, quarter, 0)

    all_rows = lax.all_gather(inputs, "rows", axis=0, tiled=True)
    wide = all_rows.astype(jnp.float32)
    total, square = group_sums(wide, GROUPS)
    act = apply_norm(wide, total, square, count, norm1_gain[0], norm1_shift[0])
    hidden = (convolve(act, conv1_weight[0], "SAME") + mine(conv1_bias[0]) + mine(extra)).astype(
        jnp.bfloat16
    )
    hidden_wide = hidden.astype(jnp.float32)
    total, square = group_sums(hidden_wide, quarter // per_group)
    act_two = apply_norm(
        hidden_wide, total, square, count, mine(norm2_gain[0]), mine(norm2_shift[0])
    )
    piece = lax.all_gather(act_two, "rows", axis=2, tiled=True)
    kernel = lax.slice_in_dim(conv2_weight[0], 0, piece.shape[2], axis=2)
    summed = jnp.zeros((full, width, quarter), jnp.float32) + convolve(piece, kernel, "SAME")
    own_part = lax.dynamic_slice_in_dim(wide, first, quarter, 2)
    partial_block = own_part + summed + mine(conv2_bias[0])
    block = lax.all_to_all(
        as_sent(partial_block), "rows", split_axis=0, concat_axis=2, tiled=True
    ).astype(partial_block.dtype)
    own_out = block.astype(jnp.bfloat16)
    flat = own_out.reshape(-1, chans)
    control = (jnp.dot(flat, zero_weight, preferred_element_type=jnp.float32) + zero_bias).astype(
        jnp.bfloat16
    )
    arrived = from_behind(control.reshape(own_out.shape), "branch", 1)
    result = (block + arrived.astype(jnp.float32)).astype(jnp.bfloat16)
    return result[None, None]


def solution(mesh):
    placed = (
        P("batch"),
        P("batch", "branch", "rows", None, None),
        P("branch", None, None, None, "rows"),
        P("branch", None),
        P("branch", None, None, None, "rows"),
        P("branch", None),
        P("branch", None),
        P("branch", None),
        P("branch", None),
        P("branch", None),
        P("branch", None, None),
        P("branch", None, None),
        P(),
        P(),
    )
    return jax.shard_map(
        body,
        mesh=mesh,
        in_specs=placed,
        out_specs=P("batch", "branch", "rows", None, None),
        check_vma=False,
    )
```

profile of v0, /device:TPU:0, one launch (start us, length us, event | category | flops | bytes accessed | tf_op | source)
XLA Modules:
  0.0 277.2 jit_solution(17344718053500666359)
XLA Ops:
  6.5 0.0 copy-start
  6.5 0.0 all-gather.6.cloned.1.call-start
  6.5 2.4 copy.45
  9.0 0.0 all-gather.6.cloned.1.call-update
  9.0 0.0 all-gather.4.cloned.1.call-start
  9.1 0.7 reduce.10
  9.8 0.7 reduce.9
  11.2 0.1 pad_maximum_fusion
  11.3 1.6 convolution_reduce_fusion
  12.9 0.8 fusion.47
  13.7 0.1 dynamic_slice.20
  13.7 0.8 constant_dynamic-slice_fusion.3
  14.5 0.8 constant_dynamic-slice_fusion.1
  15.3 51.2 %all-gather.6.cloned.1.call-done = bf16[1,1,32,64,640]{4,2,3,1,0:T(8,128)(2,1)} async-done(((bf16[1,1,8,64,640]{4,2,3,1,0:T(8,128)(2,1)}), bf16[1,1,32,64,640]{4,2,3,1,0:T(8,128)(2,1)}) %all-gather.6.cloned.1.call-update) | async-done | bytes 2621456 | tf_op jit(solution)/shard_map/all_gather | solution.py:96
  66.5 2.2 convert_reduce_fusion
  68.7 0.1 reduce_sum.47
  68.8 2.3 fusion.2
  71.1 0.1 reduce_sum.53
  71.2 0.1 reduce_sum.51
  71.3 0.1 reduce_sum.54
  71.5 0.1 mul.94
  71.5 0.1 mul.95
  71.7 0.1 sub.40
  71.7 0.1 sub.41
  71.8 3.6 %fusion.20 = bf16[32,1,64,640]{3,0,2,1:T(8,128)(2,1)S(1)} fusion(bf16[1,1,32,64,640]{4,2,3,1,0:T(8,128)(2,1)} %all-gather.6.cloned.1.call-done, f32[640]{0:T(1024)S(1)} %reduce.10, f32[640]{0:T(1024)S(1)} %reduce.9, f32[640]{0:T(1024)S(1)} %mul.95, f32[640]{0:T(1024)S(1)} %sub.41), kind=kLoop, calls=%fused_computation.25 | loop fusion | flops 13107200 | bytes 5253120 | tf_op jit(solution)/shard_map/broadcast_in_dim | solution.py:58
  75.4 0.2 pad
  75.7 0.0 copy-start.4
  75.7 1.0 copy.47
  76.7 0.2 slice.4
  76.9 9.7 %fusion.21 = (f32[160]{0:T(256)S(1)}, f32[160]{0:T(256)S(1)}, f32[32,8,9,160]{3,1,2,0:T(8,128)}) fusion(pred[8,9]{0,1:T(8,128)(4,1)S(1)} %copy-done.4, f32[160]{0:T(256)S(1)} %dynamic_slice.20, f32[160]{0:T(256)S(1)} %bitcast.96, bf16[1,3,3,640,160]{3,4,2,1,0:T(8,128)(2,1)S(1)} %copy-done, bf16[32,1,7,2,640]{4,2,3,0,1:T(8,128)(2,1)S(1)} %slice.4, ...), kind=kOutput, calls=%fused_computation.26 | convolution fusion | flops 4172758528 | bytes 6842952 | tf_op jit(solution)/shard_map/conv_general_dilated | solution.py:57
  86.5 0.1 reduce_sum.59
  86.6 0.1 reduce_sum.72
  86.7 0.1 reduce_sum.74
  86.8 0.1 reduce_sum.75
  86.9 0.1 mul.107
  87.0 0.1 mul.108
  87.1 0.1 sub.45
  87.2 0.1 sub.46
  87.2 2.4 copy.48
  89.7 0.8 multiply_convert_fusion.1
  90.5 2.8 %copy.49 = bf16[32,64,160]{1,0,2:T(8,128)(2,1)} copy(bf16[32,64,160]{2,0,1:T(8,128)(2,1)S(1)} %multiply_convert_fusion.1) | data formatting | bytes 1310720 | tf_op jit(solution)/shard_map/convert_element_type | solution.py:53
  93.3 0.0 all-gather.4.cloned.1.call-update
  93.3 0.8 constant_dynamic-slice_fusion
  94.1 4.8 %convert_element_type.66 = f32[1,1,32,64,640]{4,2,3,1,0:T(8,128)} convert(bf16[1,1,32,64,640]{4,2,3,1,0:T(8,128)(2,1)} %all-gather.6.cloned.1.call-done) | non-fusion elementwise | flops 1310720 | bytes 7864320 | tf_op jit(solution)/shard_map/convert_element_type | solution.py:97
  98.8 91.3 %all-gather.4.cloned.1.call-done = bf16[32,64,640]{1,0,2:T(8,128)(2,1)} async-done(((bf16[32,64,160]{1,0,2:T(8,128)(2,1)}), bf16[32,64,640]{1,0,2:T(8,128)(2,1)}) %all-gather.4.cloned.1.call-update) | async-done | bytes 2621456 | tf_op jit(solution)/shard_map/all_gather | solution.py:108
  190.2 10.0 %copy.50 = bf16[32,64,640]{2,0,1:T(8,128)(2,1)} copy(bf16[32,64,640]{1,0,2:T(8,128)(2,1)} %all-gather.4.cloned.1.call-done) | data formatting | bytes 5242880 | tf_op jit(solution)/shard_map/all_gather | solution.py:108
  200.2 2.0 pad.2
  202.2 0.0 copy-start.2
  202.2 1.0 copy.52
  203.2 0.2 slice.6
  203.4 0.3 copy-done.2
  203.7 8.4 %fusion.36 = f32[32,8,9,160]{3,1,2,0:T(8,128)S(1)} fusion(bf16[1,3,3,640,160]{3,4,2,1,0:T(8,128)(2,1)S(1)} %copy-done.2, bf16[32,1,7,2,640]{4,2,3,0,1:T(8,128)(2,1)S(1)} %slice.6, bf16[32,1,8,9,640]{4,2,3,0,1:T(8,128)(2,1)S(1)} %copy.52, pred[8,9]{0,1:T(8,128)(4,1)S(1)} %copy-done.4), kind=kOutput, calls=%fused_computation.45 | convolution fusion | flops 4169441280 | bytes 6840392 | tf_op jit(solution)/shard_map/conv_general_dilated | solution.py:57
  212.1 0.8 copy.53
  212.8 2.6 fusion.26
  215.5 0.6 copy.54
  216.0 28.4 %all_to_all.15 = bf16[32,64,160]{2,1,0:T(8,128)(2,1)S(1)} all-to-all(bf16[32,64,160]{2,1,0:T(8,128)(2,1)S(1)} %copy.54), channel_id=1, replica_groups=mesh['branch'=2,'batch'=4,'rows'=4] {'rows'}, dimensions={0} | all-to-all | bytes 1310720 | tf_op jit(solution)/shard_map/all_to_all | solution.py:113
  244.5 1.8 copy.56
  246.3 2.2 reshape.81
  248.6 2.7 fusion.46
  251.3 4.2 %collective-permute-start = (bf16[8,64,640]{2,1,0:T(8,128)(2,1)}, bf16[8,64,640]{2,1,0:T(8,128)(2,1)}, u32[]{:S(2)}, u32[]{:S(2)}) collective-permute-start(bf16[8,64,640]{2,1,0:T(8,128)(2,1)} %bitcast.24), channel_id=1, source_target_pairs={{0,16},{1,17},{2,18},{3,19},{4,20},{5,21},{6,22},{7,23},{8,24},{9,... | collective-permute-start | bytes 1966088 | tf_op jit(solution)/shard_map/ppermute | solution.py:22
  255.5 2.2 copy.55
  257.7 2.6 reshape.99
  260.3 7.9 %collective-permute-done = bf16[8,64,640]{2,1,0:T(8,128)(2,1)} collective-permute-done((bf16[8,64,640]{2,1,0:T(8,128)(2,1)}, bf16[8,64,640]{2,1,0:T(8,128)(2,1)}, u32[]{:S(2)}, u32[]{:S(2)}) %collective-permute-start) | collective-permute-done | bytes 655392 | tf_op jit(solution)/shard_map/ppermute | solution.py:22
  268.2 2.1 fusion.51
  (12 shorter events, 0.1 us)
Async XLA Ops:
  6.5 70.3 %copy-start = (bf16[1,3,3,640,160]{3,4,2,1,0:T(8,128)(2,1)S(1)}, bf16[1,3,3,640,160]{3,4,2,1,0:T(8,128)(2,1)}, u32[]{:S(2)}) copy-start(bf16[1,3,3,640,160]{3,4,2,1,0:T(8,128)(2,1)} %param.16) | copy-start | bytes 5529604
  6.5 6.4 %copy-start.1 = (bf16[1,1280,640]{2,1,0:T(8,128)(2,1)S(1)}, bf16[1,1280,640]{2,1,0:T(8,128)(2,1)}, u32[]{:S(2)}) copy-start(bf16[1,1280,640]{2,1,0:T(8,128)(2,1)} %param.25) | copy-start | bytes 4915204
  6.5 59.9 %all-gather.6.cloned.1.call-start = ((), (), s32[]{:S(2)}) async-start(), calls=%async_computation.2 | async-start | bytes 3276800 | tf_op jit(solution)/shard_map/all_gather | solution.py:96
  9.0 181.2 %all-gather.4.cloned.1.call-start = ((), (), s32[]{:S(2)}) async-start(), calls=%async_computation.1 | async-start | bytes 6553600 | tf_op jit(solution)/shard_map/all_gather | solution.py:108
  75.7 1.2 copy-start.4
  202.2 1.5 copy-start.2
  244.5 4.1 %copy-start.3 = (f32[640]{0:T(1024)S(1)}, f32[640]{0:T(1024)}, u32[]{:S(2)}) copy-start(f32[640]{0:T(1024)} %param.27) | copy-start | bytes 7684
  251.3 16.9 %collective-permute-start = (bf16[8,64,640]{2,1,0:T(8,128)(2,1)}, bf16[8,64,640]{2,1,0:T(8,128)(2,1)}, u32[]{:S(2)}, u32[]{:S(2)}) collective-permute-start(bf16[8,64,640]{2,1,0:T(8,128)(2,1)} %bitcast.24), channel_id=1, source_target_pairs={{0,16},{1,17},{2,18},{3,19},{4,20},{5,21},{6,22},{7,23},{8,24},{9,... | collective-permute-start | bytes 1966088 | tf_op jit(solution)/shard_map/ppermute | solution.py:22
Sparse Core Ops, SparseCore 0:
  9.1 57.2 all-gather.5
  93.4 96.6 all-gather.3
where the time goes:
time: 278 us; the launch traced here: 277 us
  waiting for transfers between devices  151 us (54%)
  local copies, waits for them, and re-layouts  36.1 us (13%)
  blocking collectives  28.4 us (10%)
  matrix products  23.1 us (8%)
  other arithmetic  20.4 us (7%)
  between operations  14.3 us (5%)
  starting transfers between devices  4.26 us (2%)
    all_gather x1, waiting for transfers between devices, body(): piece = lax.all_gather(act_two, 'rows', axis=2, tiled=True)  91.3 us
    all_gather x1, waiting for transfers between devices, body(): all_rows = lax.all_gather(inputs, 'rows', axis=0, tiled=True)  51.2 us
    all_to_all x1, blocking collectives, body(): lax.all_to_all(as_sent(partial_block), 'rows', split_axis=0, concat_axis=...  28.4 us
    conv_general_dilated x2, matrix products, convolve(): lax.conv_general_dilated(inputs[None], kernel, (1, 1), padding, dimension...  18 us
    all_gather x1, local copies, waits for them, and re-layouts, body(): piece = lax.all_gather(act_two, 'rows', axis=2, tiled=True)  10 us
    ppermute x1, waiting for transfers between devices, from_behind(): return lax.ppermute(x, axis, pairs)  7.94 us
  transfers between devices with their start and end apart: 3, of which 3 were waited for; matrix products, arithmetic and copies ran while one was open for 6% of the time, Pallas kernels for 0%

commit v1 on v0

v1 whole, which is shorter than its diff:
```python
import functools
import math

import jax
import jax.numpy as jnp
from jax import lax
from jax.experimental import pallas as pl
from jax.experimental.pallas import tpu as pltpu
from jax.sharding import PartitionSpec as P

GROUPS = 32
MESH = pl.DeviceIdType.MESH
F32 = jnp.float32
BF16 = jnp.bfloat16


def sinusoid(timestep, count):
    half = count // 2
    freqs = jnp.exp(-math.log(10000.0) * jnp.arange(half, dtype=F32) / half)
    angles = timestep.astype(F32)[0] * freqs
    return jnp.concatenate([jnp.cos(angles), jnp.sin(angles)])


def exact_dot(rows, weight):
    top = rows.astype(BF16)
    rest = rows - top.astype(F32)
    mid = rest.astype(BF16)
    low = (rest - mid.astype(F32)).astype(BF16)
    terms = jnp.concatenate([top.astype(F32), mid.astype(F32), low.astype(F32), jnp.zeros_like(rows)], axis=0)
    out = jnp.dot(terms.astype(BF16), weight, preferred_element_type=F32)
    size = rows.shape[0]
    return out[:size] + out[size : 2 * size] + out[2 * size : 3 * size]


def kernel(
    n,
    nb,
    count,
    feat,
    w1,
    w2,
    vec,
    waves,
    tw,
    ew,
    zw,
    member,
    out,
    wbuf,
    acts,
    halo1,
    hid,
    acc,
    stat1,
    stat2,
    shift,
    ctl,
    own_sem,
    zs,
    zr,
    ys,
    yr,
    ds_,
    dr,
    es,
    er,
    hs,
    hr,
    ss,
    sr,
    cs,
    cr,
):
    me = lax.axis_index("rows")
    bat = lax.axis_index("batch")
    bra = lax.axis_index("branch")
    rows, width, chans = feat.shape
    m = bat % 4
    hi, lo = m // 2, m % 2
    ymate = bat + 2 - 4 * hi
    dmate = bat + 1 - 2 * lo
    rounds = wbuf.shape[0] // 2

    own = [
        pltpu.make_async_copy(w, wbuf.at[pl.ds(9 * i, 9), me], own_sem.at[i])
        for i, w in enumerate((w1, w2))
    ]
    own[0].start()
    own[1].start()

    barrier = pltpu.get_barrier_semaphore()
    peers = [{"rows": (me + k) % n} for k in range(1, n)]
    peers += [{"batch": ymate}, {"batch": dmate}]
    peers += [{"branch": (bra + k) % nb} for k in range(1, nb)]
    for peer in peers:
        pl.semaphore_signal(barrier, inc=1, device_id=peer, device_id_type=MESH)
    pl.semaphore_wait(barrier, len(peers))

    def remote(src, dst, send, recv, to):
        return pltpu.make_async_remote_copy(
            src_ref=src, dst_ref=dst, send_sem=send, recv_sem=recv, device_id=to, device_id_type=MESH
        )

    def slot(r, src, high, low):
        return wbuf.at[2 * r + high, src, low]

    def z_copy(r, src, way):
        ref = slot(r, src, hi, lo)
        return remote(ref, ref, zs.at[way, r, src], zr.at[r, src], {"rows": me + 1 - 2 * way})

    def y_copy(r, src):
        ref = slot(r, src, hi, lo)
        return remote(ref, ref, ys.at[r, src], yr.at[r, src], {"batch": ymate})

    def d_copy(r, src):
        ref = slot(r, src, hi, lo)
        return remote(ref, ref, ds_.at[r, src], dr.at[r, src], {"batch": dmate})

    def e_copy(r, src):
        ref = slot(r, src, 1 - hi, lo)
        return remote(ref, ref, es.at[r, src], er.at[r, src], {"batch": dmate})

    def send_own(r):
        for way in range(2):

            @pl.when(me < n - 1 if way == 0 else me > 0)
            def _():
                z_copy(r, me, way).start()

    def each_source(fn):
        for d in range(1, n):

            @pl.when(me >= d)
            def _():
                fn(me - d, 0)

            @pl.when(me + d < n)
            def _():
                fn(me + d, 1)

    def z_step(r):
        def one(src, way):
            z_copy(r, src, way).wait_recv()

            @pl.when(me < n - 1 if way == 0 else me > 0)
            def _():
                z_copy(r, src, way).start()

            y_copy(r, src).start()
            d_copy(r, src).start()

        each_source(one)

    def y_step(r):
        def one(src, way):
            y_copy(r, src).wait_recv()
            e_copy(r, src).start()

        each_source(one)

    def d_step(r):
        def one(src, way):
            d_copy(r, src).wait_recv()
            e_copy(r, src).wait_recv()

        each_source(one)

    def drain(r):
        def one(src, way):
            @pl.when(me < n - 1 if way == 0 else me > 0)
            def _():
                z_copy(r, src, way).wait_send()

            y_copy(r, src).wait_send()
            d_copy(r, src).wait_send()
            e_copy(r, src).wait_send()

        each_source(one)
        for way in range(2):

            @pl.when(me < n - 1 if way == 0 else me > 0)
            def _():
                z_copy(r, me, way).wait_send()

    def halo(first, last, buf, k):
        up = remote(first, buf.at[rows + 1], hs.at[k, 0], hr.at[k, 0], {"rows": me - 1})
        down = remote(last, buf.at[0], hs.at[k, 1], hr.at[k, 1], {"rows": me + 1})
        return up, down

    def halo_start(pair):
        @pl.when(me > 0)
        def _():
            pair[0].start()

        @pl.when(me < n - 1)
        def _():
            pair[1].start()

    def halo_wait(pair):
        @pl.when(me < n - 1)
        def _():
            pair[0].wait_recv()
            pair[1].wait_send()

        @pl.when(me > 0)
        def _():
            pair[1].wait_recv()
            pair[0].wait_send()

    def stat_copies(buf, k):
        return [
            remote(buf.at[0], buf.at[j], ss.at[k, j], sr.at[k, j], {"rows": (me + j) % n})
            for j in range(1, n)
        ]

    def local_sums(read, buf):
        def step(i, carry):
            v = read(i).astype(F32)
            return carry[0] + jnp.sum(v, axis=0, keepdims=True), carry[1] + jnp.sum(
                v * v, axis=0, keepdims=True
            )

        zero = jnp.zeros((1, chans), F32)
        total, square = lax.fori_loop(0, rows, step, (zero, zero))
        buf[0] = jnp.concatenate([total, square, jnp.zeros((6, chans), F32)], axis=0)

    def activate(buf, stat, gain, offset):
        sums = stat[0]
        for j in range(1, n):
            sums = sums + stat[j]
        grouped = exact_dot(sums, member[...])
        mean = grouped[0:1] / count
        var = grouped[1:2] / count - mean * mean
        scale = lax.rsqrt(var + 1e-05) * gain
        base = offset - mean * scale
        col = lax.broadcasted_iota(jnp.int32, (width, chans), 0)

        def step(i, carry):
            v = buf[i].astype(F32) * scale + base
            v = v / (1.0 + jnp.exp(-v))
            row = me * rows + i
            v = jnp.where((row >= 1) & (row <= n * rows), v, 0.0)
            acts[1, i] = v.astype(BF16)
            acts[0, i] = jnp.where(col == 0, 0.0, pltpu.roll(v, 1, 0)).astype(BF16)
            acts[2, i] = jnp.where(col == width - 1, 0.0, pltpu.roll(v, width - 1, 0)).astype(BF16)
            return carry

        lax.fori_loop(0, rows + 2, step, 0)

    def taps(first, last):
        def step(t, carry):
            k = t % 9
            a = acts[k % 3, pl.ds(k // 3, rows)].reshape(rows * width, chans)
            w = wbuf[t].reshape(chans, chans)
            acc[...] += lax.dot_general(a, w, (((1,), (1,)), ((), ())), preferred_element_type=F32)
            return carry

        lax.fori_loop(first, last, step, 0)

    pair1 = halo(feat.at[0], feat.at[rows - 1], halo1, 0)
    halo_start(pair1)
    local_sums(lambda i: feat[i], stat1)
    stats1 = stat_copies(stat1, 0)
    for copy in stats1:
        copy.start()
    own[0].wait()
    own[1].wait()
    send_own(0)
    send_own(1)

    inner = exact_dot(jnp.broadcast_to(waves[...], (8, waves.shape[1])), tw[...])
    inner = inner / (1.0 + jnp.exp(-inner))
    shift[...] = exact_dot(inner, ew[...])
    acc[...] = jnp.zeros_like(acc)
    for i in range(rows):
        halo1[i + 1] = feat[i]

    def begin():
        halo_wait(pair1)
        for copy in stats1:
            copy.wait()
        activate(halo1, stat1, vec[2:3], vec[3:4])

    pair2 = halo(hid.at[1], hid.at[rows], hid, 1)
    stats2 = stat_copies(stat2, 1)

    def middle():
        bias = vec[0:1] + shift[0:1]

        def step(i, carry):
            at = pl.ds(pl.multiple_of(i * width, width), width)
            hid[i + 1] = (acc[at, :] + bias).astype(BF16)
            acc[at, :] = jnp.zeros((width, chans), F32)
            return carry

        lax.fori_loop(0, rows, step, 0)
        local_sums(lambda i: hid[i + 1], stat2)
        for copy in stats2:
            copy.start()
        halo_start(pair2)

    def second():
        halo_wait(pair2)
        for copy in stats2:
            copy.wait()
        activate(hid, stat2, vec[4:5], vec[5:6])

    for s in range(rounds + 2):
        if s < rounds:
            if 2 <= s + 1 < rounds:
                send_own(s + 1)
            z_step(s)
        if 0 <= s - 1 < rounds:
            y_step(s - 1)
        r = s - 2
        if r == -1:
            begin()
        if r >= 0:
            d_step(r)
            if r < 4:
                taps(2 * r, 2 * r + 2)
            elif r == 4:
                taps(8, 9)
                middle()
            elif r == 5:
                second()
                taps(9, 12)
            else:
                taps(2 * r, 2 * r + 2)

    def ctl_copy(i):
        return remote(out.at[0, 0, pl.ds(2 * i, 2)], ctl.at[pl.ds(2 * i, 2)], cs.at[i], cr.at[i], {"branch": bra + 1})

    @pl.when(bra == 0)
    def _():
        for i in range(rows // 2):
            for k in range(2 * i, 2 * i + 2):
                out[0, 0, k] = (feat[k].astype(F32) + acc[k * width : (k + 1) * width, :] + vec[1:2]).astype(BF16)
            ctl_copy(i).start()
        for i in range(rows // 2):
            ctl_copy(i).wait_send()

    @pl.when(bra == 1)
    def _():
        for i in range(rows // 2):
            ctl_copy(i).wait_recv()
            got = ctl[2 * i : 2 * i + 2].reshape(2 * width, chans)
            res = (jnp.dot(got, zw[...], preferred_element_type=F32) + vec[6:7]).astype(BF16).astype(F32)
            x = feat[2 * i : 2 * i + 2].reshape(2 * width, chans).astype(F32)
            y = x + acc[2 * i * width : (2 * i + 2) * width, :] + vec[1:2] + res
            out[0, 0, pl.ds(2 * i, 2)] = y.astype(BF16).reshape(2, width, chans)

    for r in range(rounds):
        drain(r)


def body(n, nb, *args):
    (timestep, features, w1, b1, w2, b2, g1, s1, g2, s2, tw, ew, zw, zb) = args
    feat = features[0, 0]
    rows, width, chans = feat.shape
    per_group = chans // GROUPS
    count = float(rows * n * width * per_group)
    quarter = w1.shape[4]

    def turned(w):
        return jnp.swapaxes(w[0].reshape(9, chans, quarter), 1, 2).reshape(9, 2, quarter // 2, chans)

    vec = jnp.concatenate([b1, b2, g1, s1, g2, s2, zb[None], jnp.zeros_like(b1)], axis=0)
    waves = sinusoid(timestep, tw.shape[1])[None]
    group = jnp.arange(chans) // per_group
    member = (group[:, None] == group[None, :]).astype(BF16)
    rounds = 9
    dma = pltpu.SemaphoreType.DMA
    vmem = pl.BlockSpec(memory_space=pltpu.VMEM)
    anyspace = pl.BlockSpec(memory_space=pl.ANY)
    return pl.pallas_call(
        functools.partial(kernel, n, nb, count),
        out_shape=jax.ShapeDtypeStruct(features.shape, BF16),
        in_specs=[vmem, anyspace, anyspace] + [vmem] * 6,
        out_specs=vmem,
        scratch_shapes=[
            pltpu.VMEM((18, n, 2, quarter // 2, chans), BF16),
            pltpu.VMEM((3, rows + 2, width, chans), BF16),
            pltpu.VMEM((rows + 2, width, chans), BF16),
            pltpu.VMEM((rows + 2, width, chans), BF16),
            pltpu.VMEM((rows * width, chans), F32),
            pltpu.VMEM((n, 8, chans), F32),
            pltpu.VMEM((n, 8, chans), F32),
            pltpu.VMEM((8, chans), F32),
            pltpu.VMEM((rows, width, chans), BF16),
            dma((2,)),
            dma((2, rounds, n)),
            dma((rounds, n)),
            dma((rounds, n)),
            dma((rounds, n)),
            dma((rounds, n)),
            dma((rounds, n)),
            dma((rounds, n)),
            dma((rounds, n)),
            dma((2, 2)),
            dma((2, 2)),
            dma((2, n)),
            dma((2, n)),
            dma((rows // 2,)),
            dma((rows // 2,)),
        ],
        compiler_params=pltpu.CompilerParams(
            collective_id=0, has_side_effects=True, vmem_limit_bytes=60 * 1024 * 1024
        ),
    )(feat, turned(w1), turned(w2), vec, waves, tw[0], ew[0], zw, member)


def solution(mesh):
    placed = (
        P("batch"),
        P("batch", "branch", "rows", None, None),
        P("branch", None, None, None, "rows"),
        P("branch", None),
        P("branch", None, None, None, "rows"),
        P("branch", None),
        P("branch", None),
        P("branch", None),
        P("branch", None),
        P("branch", None),
        P("branch", None, None),
        P("branch", None, None),
        P(),
        P(),
    )
    return jax.shard_map(
        functools.partial(body, mesh.shape["rows"], mesh.shape["branch"]),
        mesh=mesh,
        in_specs=placed,
        out_specs=P("batch", "branch", "rows", None, None),
        check_vma=False,
    )
```

time: 278 us -> 115 us (0.41)
  waiting for transfers between devices: 151 us -> 0 us
  Pallas kernels: 0 us -> 108 us
  local copies, waits for them, and re-layouts: 36.1 us -> 4.66 us
  blocking collectives: 28.4 us -> 0 us
  matrix products: 23.1 us -> 0 us
  other arithmetic: 20.4 us -> 1.24 us
  between operations: 14.3 us -> 0.68 us
  starting transfers between devices: 4.26 us -> 0 us
    all_gather x2 -> x0, waiting for transfers between devices: 143 us -> none  [the longest x1 91.3 us: body(): piece = lax.all_gather(act_two, 'rows', axis=2, tiled=True)]
    pallas_call x0 -> x1, Pallas kernels: none -> 108 us  [body(): pl.pallas_call(functools.partial(kernel, n, nb, count), out_shape=jax.Sha...]
    all_to_all x1 -> x0, blocking collectives: 28.4 us -> none  [body(): lax.all_to_all(as_sent(partial_block), 'rows', split_axis=0, concat_axis=...]
    conv_general_dilated x2 -> x0, matrix products: 18 us -> none  [convolve(): lax.conv_general_dilated(inputs[None], kernel, (1, 1), padding, dimension...]
    all_gather x1 -> x0, local copies, waits for them, and re-layouts: 10 us -> none  [body(): piece = lax.all_gather(act_two, 'rows', axis=2, tiled=True)]
    convert_element_type x4 -> x0, local copies, waits for them, and re-layouts: 8.16 us -> none  [the longest x2 4.78 us: body(): block = lax.all_to_all(as_sent(partial_block), 'rows', split_axis=0, conc...]
    ppermute x1 -> x0, waiting for transfers between devices: 7.94 us -> none  [from_behind(): return lax.ppermute(x, axis, pairs)]
    convert_element_type x3 -> x1, other arithmetic: 8.17 us -> 1.11 us  [body(): member = (group[:, None] == group[None, :]).astype(BF16)]
  transfers between devices with their start and end apart: 3 -> 0, of which waited for: 3 -> 0; matrix products, arithmetic and copies ran while one was open for 6% -> 0% of each run, Pallas kernels for 0% -> 0%
where the time goes in v1:
time: 115 us
  Pallas kernels  108 us (94%)
  local copies, waits for them, and re-layouts  4.66 us (4%)
  other arithmetic  1.24 us (1%)
    pallas_call x1, Pallas kernels, body(): pl.pallas_call(functools.partial(kernel, n, nb, count), out_shape=jax.Sha...  108 us

profile of v1, /device:TPU:0, one launch (start us, length us, event | category | flops | bytes accessed | tf_op | source)
XLA Modules:
  0.0 114.8 jit_solution(16335022455508871928)
XLA Ops:
  0.7 0.1 pad_maximum_fusion
  0.8 0.6 broadcast_in_dim.13.waves
  1.4 0.7 broadcast_in_dim.11
  2.1 1.4 %concatenate.6.vec = f32[8,640]{1,0:T(8,128)} concatenate(f32[1,640]{1,0:T(1,128)} %param.17, f32[1,640]{1,0:T(1,128)} %param.19, f32[1,640]{1,0:T(1,128)} %param.20, f32[1,640]{1,0:T(1,128)} %param.21, f32[1,640]{1,0:T(1,128)} %param.22, f32[1,640]{1,0:T(1,128)} %param.23, f32[1,640]{1,0:T(1,128)S(1)} %broadcast_in_dim.11, f32[1,640]{1,0:T(1,128)S(1)} %broadcast_in_dim.12), dimensions={0} | concatenate | bytes 40960 | tf_op jit(solution)/shard_map/concatenate | solution.py:368
  3.5 1.1 compare_convert_fusion.member
  4.6 108.2 %shard_map.136 = bf16[1,1,8,64,640]{4,3,2,1,0:T(8,128)(2,1)} custom-call(bf16[8,64,640]{2,1,0:T(8,128)(2,1)} %bitcast.18, bf16[9,2,80,640]{3,2,1,0:T(8,128)(2,1)} %bitcast.14, bf16[9,2,80,640]{3,2,1,0:T(8,128)(2,1)} %bitcast.15, f32[8,640]{1,0:T(8,128)} %concatenate.6.vec, f32[1,320]{1,0:T(1,128)} %broadcast_in_dim.13.waves, bf16[320,1280]{1,0:T(8,128)(2,1)} %bitcast.17, ...), custom_call_target="tpu_custom_call" | custom-call | tf_op jit(solution)/shard_map/pallas_call | solution.py:376
  112.8 2.0 %copy.17 = bf16[1,1,8,64,640]{4,3,2,1,0:T(8,128)(2,1)} copy(bf16[1,1,8,64,640]{4,3,2,1,0:T(8,128)(2,1)} %shard_map.136) | data formatting | bytes 1310720
  (3 shorter events, 0.1 us)

commit v2 on v1

--- a/solution.py
+++ b/solution.py
@@ -9,6 +9,8 @@
 from jax.sharding import PartitionSpec as P
 
 GROUPS = 32
+LEAD = 2
+SKEW = 1
 MESH = pl.DeviceIdType.MESH
 F32 = jnp.float32
 BF16 = jnp.bfloat16
@@ -39,13 +41,22 @@
     feat,
     w1,
     w2,
-    vec,
+    b1,
+    b2,
+    g1,
+    s1,
+    g2,
+    s2,
+    zb,
     waves,
+    tw_hbm,
+    ew_hbm,
+    zw_hbm,
+    out,
     tw,
     ew,
     zw,
     member,
-    out,
     wbuf,
     acts,
     halo1,
@@ -87,6 +98,10 @@
     ]
     own[0].start()
     own[1].start()
+    extra = [
+        pltpu.make_async_copy(a, b, own_sem.at[2 + i])
+        for i, (a, b) in enumerate(((tw_hbm, tw), (ew_hbm, ew), (zw_hbm, zw)))
+    ]
 
     barrier = pltpu.get_barrier_semaphore()
     peers = [{"rows": (me + k) % n} for k in range(1, n)]
@@ -127,18 +142,20 @@
             def _():
                 z_copy(r, me, way).start()
 
+    def at_distance(fn, d):
+        @pl.when(me >= d)
+        def _():
+            fn(me - d, 0)
+
+        @pl.when(me + d < n)
+        def _():
+            fn(me + d, 1)
+
     def each_source(fn):
         for d in range(1, n):
-
-            @pl.when(me >= d)
-            def _():
-                fn(me - d, 0)
-
-            @pl.when(me + d < n)
-            def _():
-                fn(me + d, 1)
-
-    def z_step(r):
+            at_distance(fn, d)
+
+    def z_step(r, d):
         def one(src, way):
             z_copy(r, src, way).wait_recv()
 
@@ -149,14 +166,14 @@
             y_copy(r, src).start()
             d_copy(r, src).start()
 
-        each_source(one)
-
-    def y_step(r):
+        at_distance(one, d)
+
+    def y_step(r, d):
         def one(src, way):
             y_copy(r, src).wait_recv()
             e_copy(r, src).start()
 
-        each_source(one)
+        at_distance(one, d)
 
     def d_step(r):
         def one(src, way):
@@ -259,33 +276,42 @@
 
     pair1 = halo(feat.at[0], feat.at[rows - 1], halo1, 0)
     halo_start(pair1)
+    own[0].wait()
+    for r in range(LEAD):
+        send_own(r)
+    for copy in extra:
+        copy.start()
     local_sums(lambda i: feat[i], stat1)
     stats1 = stat_copies(stat1, 0)
     for copy in stats1:
         copy.start()
-    own[0].wait()
-    own[1].wait()
-    send_own(0)
-    send_own(1)
-
-    inner = exact_dot(jnp.broadcast_to(waves[...], (8, waves.shape[1])), tw[...])
-    inner = inner / (1.0 + jnp.exp(-inner))
-    shift[...] = exact_dot(inner, ew[...])
+    per_group = chans // GROUPS
+    low = lax.broadcasted_iota(jnp.int32, (chans, chans), 0)
+    high = lax.broadcasted_iota(jnp.int32, (chans, chans), 1)
+    same = jnp.floor((low.astype(F32) + 0.5) / per_group) == jnp.floor((high.astype(F32) + 0.5) / per_group)
+    member[...] = jnp.where(same, 1.0, 0.0).astype(BF16)
     acc[...] = jnp.zeros_like(acc)
     for i in range(rows):
         halo1[i + 1] = feat[i]
+
+    def time_shift():
+        extra[0].wait()
+        extra[1].wait()
+        inner = exact_dot(jnp.broadcast_to(waves[...], (8, waves.shape[1])), tw[...])
+        inner = inner / (1.0 + jnp.exp(-inner))
+        shift[...] = exact_dot(inner, ew[...])
 
     def begin():
         halo_wait(pair1)
         for copy in stats1:
             copy.wait()
-        activate(halo1, stat1, vec[2:3], vec[3:4])
+        activate(halo1, stat1, g1[...], s1[...])
 
     pair2 = halo(hid.at[1], hid.at[rows], hid, 1)
     stats2 = stat_copies(stat2, 1)
 
     def middle():
-        bias = vec[0:1] + shift[0:1]
+        bias = b1[...] + shift[0:1]
 
         def step(i, carry):
             at = pl.ds(pl.multiple_of(i * width, width), width)
@@ -303,30 +329,37 @@
         halo_wait(pair2)
         for copy in stats2:
             copy.wait()
-        activate(hid, stat2, vec[4:5], vec[5:6])
-
-    for s in range(rounds + 2):
-        if s < rounds:
-            if 2 <= s + 1 < rounds:
-                send_own(s + 1)
-            z_step(s)
-        if 0 <= s - 1 < rounds:
-            y_step(s - 1)
-        r = s - 2
-        if r == -1:
-            begin()
-        if r >= 0:
-            d_step(r)
-            if r < 4:
-                taps(2 * r, 2 * r + 2)
-            elif r == 4:
-                taps(8, 9)
-                middle()
-            elif r == 5:
-                second()
-                taps(9, 12)
-            else:
-                taps(2 * r, 2 * r + 2)
+        activate(hid, stat2, g2[...], s2[...])
+
+    def tap(t):
+        return lambda: taps(t, t + 1)
+
+    lag = 2 + SKEW * (n - 2)
+    plan = {0: [time_shift], 1: [begin]}
+    for r in range(rounds):
+        plan[r + lag] = [tap(2 * r), tap(2 * r + 1)]
+    plan[4 + lag] = [tap(8), middle]
+    plan[5 + lag] = [second, tap(9), tap(10), tap(11)]
+    for s in range(rounds + lag):
+        nxt = s + LEAD
+        if nxt < rounds:
+            if nxt == max(LEAD, 4):
+                own[1].wait()
+            send_own(nxt)
+        if s >= lag:
+            d_step(s - lag)
+        work = list(plan.get(s, []))
+        for d in range(1, n):
+            r = s - SKEW * (d - 1)
+            if 0 <= r < rounds:
+                z_step(r, d)
+            if 0 <= r - 1 < rounds:
+                y_step(r - 1, d)
+            if work:
+                work.pop(0)()
+        for unit in work:
+            unit()
+    extra[2].wait()
 
     def ctl_copy(i):
         return remote(out.at[0, 0, pl.ds(2 * i, 2)], ctl.at[pl.ds(2 * i, 2)], cs.at[i], cr.at[i], {"branch": bra + 1})
@@ -335,7 +368,7 @@
     def _():
         for i in range(rows // 2):
             for k in range(2 * i, 2 * i + 2):
-                out[0, 0, k] = (feat[k].astype(F32) + acc[k * width : (k + 1) * width, :] + vec[1:2]).astype(BF16)
+                out[0, 0, k] = (feat[k].astype(F32) + acc[k * width : (k + 1) * width, :] + b2[...]).astype(BF16)
             ctl_copy(i).start()
         for i in range(rows // 2):
             ctl_copy(i).wait_send()
@@ -345,9 +378,9 @@
         for i in range(rows // 2):
             ctl_copy(i).wait_recv()
             got = ctl[2 * i : 2 * i + 2].reshape(2 * width, chans)
-            res = (jnp.dot(got, zw[...], preferred_element_type=F32) + vec[6:7]).astype(BF16).astype(F32)
+            res = (jnp.dot(got, zw[...], preferred_element_type=F32) + zb[...]).astype(BF16).astype(F32)
             x = feat[2 * i : 2 * i + 2].reshape(2 * width, chans).astype(F32)
-            y = x + acc[2 * i * width : (2 * i + 2) * width, :] + vec[1:2] + res
+            y = x + acc[2 * i * width : (2 * i + 2) * width, :] + b2[...] + res
             out[0, 0, pl.ds(2 * i, 2)] = y.astype(BF16).reshape(2, width, chans)
 
     for r in range(rounds):
@@ -365,10 +398,7 @@
     def turned(w):
         return jnp.swapaxes(w[0].reshape(9, chans, quarter), 1, 2).reshape(9, 2, quarter // 2, chans)
 
-    vec = jnp.concatenate([b1, b2, g1, s1, g2, s2, zb[None], jnp.zeros_like(b1)], axis=0)
     waves = sinusoid(timestep, tw.shape[1])[None]
-    group = jnp.arange(chans) // per_group
-    member = (group[:, None] == group[None, :]).astype(BF16)
     rounds = 9
     dma = pltpu.SemaphoreType.DMA
     vmem = pl.BlockSpec(memory_space=pltpu.VMEM)
@@ -376,9 +406,13 @@
     return pl.pallas_call(
         functools.partial(kernel, n, nb, count),
         out_shape=jax.ShapeDtypeStruct(features.shape, BF16),
-        in_specs=[vmem, anyspace, anyspace] + [vmem] * 6,
+        in_specs=[vmem, anyspace, anyspace] + [vmem] * 8 + [anyspace] * 3,
         out_specs=vmem,
         scratch_shapes=[
+            pltpu.VMEM(tw.shape[1:], BF16),
+            pltpu.VMEM(ew.shape[1:], BF16),
+            pltpu.VMEM(zw.shape, BF16),
+            pltpu.VMEM((chans, chans), BF16),
             pltpu.VMEM((18, n, 2, quarter // 2, chans), BF16),
             pltpu.VMEM((3, rows + 2, width, chans), BF16),
             pltpu.VMEM((rows + 2, width, chans), BF16),
@@ -388,7 +422,7 @@
             pltpu.VMEM((n, 8, chans), F32),
             pltpu.VMEM((8, chans), F32),
             pltpu.VMEM((rows, width, chans), BF16),
-            dma((2,)),
+            dma((5,)),
             dma((2, rounds, n)),
             dma((rounds, n)),
             dma((rounds, n)),
@@ -407,7 +441,7 @@
         compiler_params=pltpu.CompilerParams(
             collective_id=0, has_side_effects=True, vmem_limit_bytes=60 * 1024 * 1024
         ),
-    )(feat, turned(w1), turned(w2), vec, waves, tw[0], ew[0], zw, member)
+    )(feat, turned(w1), turned(w2), b1, b2, g1, s1, g2, s2, zb[None], waves, tw[0], ew[0], zw)
 
 
 def solution(mesh):

time: 115 us -> 107 us (0.930)
  Pallas kernels: 108 us -> 102 us
    pallas_call x1, Pallas kernels: 108 us -> 102 us  [body(): pl.pallas_call(functools.partial(kernel, n, nb, count), out_shape=jax.Sha...]
    concatenate x1 -> x0, local copies, waits for them, and re-layouts: 1.4 us -> none  [body(): jnp.concatenate([b1, b2, g1, s1, g2, s2, zb[None], jnp.zeros_like(b1)], a...]
where the time goes in v2:
time: 107 us; the launch traced here: 106 us
  Pallas kernels  102 us (95%)
  local copies, waits for them, and re-layouts  3.82 us (4%)
    pallas_call x1, Pallas kernels, body(): pl.pallas_call(functools.partial(kernel, n, nb, count), out_shape=jax.Sha...  102 us

profile of v2, /device:TPU:0, one launch (start us, length us, event | category | flops | bytes accessed | tf_op | source)
XLA Modules:
  0.0 106.3 jit_solution(13463891397606836080)
XLA Ops:
  0.7 0.1 pad_maximum_fusion
  0.8 0.6 broadcast_in_dim.7.waves
  1.4 1.3 %broadcast_in_dim.6.zb = f32[1,640]{1,0:T(1,128)} reshape(f32[640]{0:T(1024)} %param.27) | data formatting | bytes 5120 | tf_op jit(solution)/shard_map/broadcast_in_dim | solution.py:444
  2.6 101.7 %shard_map.136 = bf16[1,1,8,64,640]{4,3,2,1,0:T(8,128)(2,1)} custom-call(bf16[8,64,640]{2,1,0:T(8,128)(2,1)} %bitcast.18, bf16[9,2,80,640]{3,2,1,0:T(8,128)(2,1)} %bitcast.14, bf16[9,2,80,640]{3,2,1,0:T(8,128)(2,1)} %bitcast.15, f32[1,640]{1,0:T(1,128)} %b1.1, f32[1,640]{1,0:T(1,128)} %b2.1, f32[1,640]{1,0:T(1,128)} %g1.1, f32[1,640]{1,0:T(1,128)} %s1_.1, ...), custom_call_target="tpu_custom_call" | custom-call | tf_op jit(solution)/shard_map/pallas_call | solution.py:406
  104.3 2.0 %copy.17 = bf16[1,1,8,64,640]{4,3,2,1,0:T(8,128)(2,1)} copy(bf16[1,1,8,64,640]{4,3,2,1,0:T(8,128)(2,1)} %shard_map.136) | data formatting | bytes 1310720
  (1 shorter events, 0.0 us)
